TPU v7x, 8 devices: a whole 2x2x1 slice. The times are simulated.
8 devices in a mesh: dp: 2 (over z, y), tp: 4 (over x, core).
Axes of the slice: x: 2, y: 2, z: 1, core: 2. Of those that a mesh axis runs over, the one named last changes fastest.
Arguments:
- x: bfloat16 [12, 2048, 3072], P('dp'), parts along dimension 0
- gamma: float32 [3072], replicated
- beta: float32 [3072], replicated
- wq: bfloat16 [3072, 4096], P(None, 'tp')
- wkv: bfloat16 [3072, 512], replicated
- wo: bfloat16 [4096, 3072], P('tp')
- w1: bfloat16 [3072, 24576], P(None, 'tp')
- w3: bfloat16 [3072, 24576], P(None, 'tp')
- w2: bfloat16 [24576, 3072], P('tp')
Outputs:
- output: bfloat16 [12, 2048, 3072], P('dp'), parts along dimension 0
There are 2 independent parts. A program takes and returns all parts, laid end to end along the dimension named above; an argument that names none is the same for every part.
All inputs are finite; a program needn't handle non-finite values.
Results may differ from a plain program's by a relative error of at most 0.0107695.
Values are sent between devices in bfloat16 or wider.
A program may use at most 1.25 GiB of HBM per device.

v0:
```python
import jax
import jax.numpy as jnp
from jax import lax
from jax.sharding import PartitionSpec as P

EPS = 1e-5


def solution(mesh):
    def local(x, gamma, beta, wq, wkv, wo, w1, w3, w2):
        b, s, d = x.shape
        dh = wkv.shape[1] // 2
        nh = wq.shape[1] // dh
        xf = x.astype(jnp.float32)
        mu = jnp.mean(xf, axis=-1, keepdims=True)
        var = jnp.mean(jnp.square(xf - mu), axis=-1, keepdims=True)
        ln = ((xf - mu) * lax.rsqrt(var + EPS) * gamma + beta).astype(jnp.bfloat16).reshape(b * s, d)
        q = jnp.dot(ln, wq, preferred_element_type=jnp.float32).astype(jnp.bfloat16).reshape(b, s, nh, dh)
        kv = jnp.dot(ln, wkv, preferred_element_type=jnp.float32).astype(jnp.bfloat16).reshape(b, s, 2 * dh)
        k = kv[:, :, :dh]
        v = kv[:, :, dh:]
        sc = jnp.einsum('bqhe,bke->bhqk', q, k, preferred_element_type=jnp.float32) * dh ** -0.5
        qi = lax.broadcasted_iota(jnp.int32, (s, s), 0)
        ki = lax.broadcasted_iota(jnp.int32, (s, s), 1)
        sc = jnp.where(ki <= qi, sc, -1e30)
        p = jax.nn.softmax(sc, axis=-1).astype(jnp.bfloat16)
        o = jnp.einsum('bhqk,bke->bqhe', p, v, preferred_element_type=jnp.float32).astype(jnp.bfloat16).reshape(b * s, nh * dh)
        a = jnp.dot(o, wo, preferred_element_type=jnp.float32)
        g = jnp.dot(ln, w1, preferred_element_type=jnp.float32)
        u = jnp.dot(ln, w3, preferred_element_type=jnp.float32)
        hm = (jax.nn.silu(g) * u).astype(jnp.bfloat16)
        m = jnp.dot(hm, w2, preferred_element_type=jnp.float32)
        part = (a + m).astype(jnp.bfloat16)
        tot = lax.psum(part, 'tp')
        return (xf + tot.astype(jnp.float32).reshape(b, s, d)).astype(jnp.bfloat16)

    return jax.shard_map(local, mesh=mesh,
                         in_specs=(P('dp', None, None), P(), P(), P(None, 'tp'), P(), P('tp', None),
                                   P(None, 'tp'), P(None, 'tp'), P('tp', None)),
                         out_specs=P('dp', None, None), check_vma=False)
```

profile of v0, /device:TPU:0, one launch (start us, length us, event | category | flops | bytes accessed | tf_op | source)
XLA Modules:
  0.0 3581.8 jit_solution(14519870028983084599)
XLA Ops:
  6.5 0.0 copy-start
  6.5 0.0 all-reduce.2.cloned.1.call-start
  6.5 4.1 iota_compare_fusion
  10.6 0.0 copy-start.2
  10.6 0.0 copy-start.3
  10.6 23.4 convert_reduce_fusion
  34.1 27.2 fusion.8
  61.3 0.0 copy-done.2
  61.3 0.0 copy-done.3
  61.3 49.6 %fusion.11 = bf16[6,2048,3072]{2,1,0:T(8,128)(2,1)} fusion(bf16[6,2048,3072]{2,1,0:T(8,128)(2,1)} %param.9, f32[3072]{0:T(1024)S(1)} %copy-done.2, f32[3072]{0:T(1024)S(1)} %copy-done.3, f32[6,2048]{1,0:T(8,128)S(1)} %add_rsqrt_fusion, f32[6,2048]{1,0:T(8,128)S(1)} %broadcast_multiply_fusion), kind=kLoop, calls=%fused_computation.18 | loop fusion | flops 226492416 | bytes 151117824 | tf_op jit(solution)/shard_map/convert_element_type | solution.py:17
  110.9 0.0 copy-done
  110.9 48.0 %convolution_convert_fusion.1 = bf16[12288,512]{1,0:T(8,128)(2,1)} fusion(bf16[12288,3072]{1,0:T(8,128)(2,1)} %bitcast, bf16[3072,512]{1,0:T(8,128)(2,1)S(1)} %copy-done), kind=kOutput, calls=%fused_computation.28 | convolution fusion | flops 38660997120 | bytes 91226112 | tf_op jit(solution)/shard_map/dot_general | solution.py:19
  158.9 87.5 %convolution_convert_fusion = bf16[12288,1024]{1,0:T(8,128)(2,1)} fusion(bf16[12288,3072]{1,0:T(8,128)(2,1)} %bitcast, bf16[3072,1024]{1,0:T(8,128)(2,1)} %param.12), kind=kOutput, calls=%fused_computation.24 | convolution fusion | flops 77321994240 | bytes 106954752 | tf_op jit(solution)/shard_map/dot_general | solution.py:18
  246.4 41.2 %reshape.36 = bf16[6,2048,4,256]{3,2,1,0:T(4,128)(2,1)} reshape(bf16[12288,1024]{1,0:T(8,128)(2,1)} %convolution_convert_fusion) | data formatting | bytes 50331648 | tf_op jit(solution)/shard_map/reshape | solution.py:18
  287.7 184.4 %fusion.26 = (f32[6,4,2048]{2,1,0:T(4,128)S(1)}, f32[6,4,2048,2048]{2,3,1,0:T(8,128)}) fusion(pred[2048,2048]{0,1:T(8,128)(4,1)} %iota_compare_fusion, bf16[6,2048,4,256]{3,2,1,0:T(4,128)(2,1)} %reshape.36, bf16[6,2048,512]{2,1,0:T(8,128)(2,1)} %bitcast.53), kind=kOutput, calls=%fused_computation.37 | convolution fusion | flops 51942260736 | bytes 438501376 | tf_op jit(solution)/shard_map/sub | solution.py:26
  472.1 130.1 %convert_bitcast_fusion = bf16[6,2048,4,256]{1,3,2,0:T(8,128)(2,1)} fusion(f32[6,4,2048,2048]{2,3,1,0:T(8,128)} %get-tuple-element.6, f32[6,4,2048]{2,1,0:T(4,128)S(1)} %get-tuple-element.5, bf16[6,2048,512]{2,1,0:T(8,128)(2,1)} %bitcast.54), kind=kOutput, calls=%fused_computation.23 | convolution fusion | flops 51753517056 | bytes 434307072 | tf_op jit(solution)/shard_map/bhqk,bke->bqhe/dot_general | solution.py:27
  602.2 38.3 %copy.16 = bf16[6,2048,4,256]{3,2,1,0:T(4,128)(2,1)} copy(bf16[6,2048,4,256]{1,3,2,0:T(8,128)(2,1)} %convert_bitcast_fusion) | data formatting | bytes 50331648 | tf_op jit(solution)/shard_map/convert_element_type | solution.py:27
  640.5 24.8 copy.22
  665.3 488.2 %fusion.31 = f32[12288,6144]{1,0:T(8,128)} fusion(bf16[12288,3072]{1,0:T(8,128)(2,1)} %bitcast, bf16[3072,6144]{1,0:T(8,128)(2,1)} %param.15), kind=kOutput, calls=%fused_computation.38 | convolution fusion | flops 463856467968 | bytes 415236096 | tf_op jit(solution)/shard_map/dot_general | solution.py:29
  1153.6 488.5 %fusion.32 = f32[12288,6144]{1,0:T(8,128)} fusion(bf16[12288,3072]{1,0:T(8,128)(2,1)} %bitcast, bf16[3072,6144]{1,0:T(8,128)(2,1)} %param.16), kind=kOutput, calls=%fused_computation.39 | convolution fusion | flops 463856467968 | bytes 415236096 | tf_op jit(solution)/shard_map/dot_general | solution.py:30
  1642.0 533.8 %fusion.13 = f32[12288,3072]{1,0:T(8,128)} fusion(bf16[6144,3072]{1,0:T(8,128)(2,1)} %param.17, f32[12288,6144]{1,0:T(8,128)} %fusion.32, f32[12288,6144]{1,0:T(8,128)} %fusion.31), kind=kOutput, calls=%fused_computation.21 | convolution fusion | flops 464309452800 | bytes 792723456 | tf_op jit(solution)/shard_map/dot_general | solution.py:32
  2175.8 94.6 %add_convert_fusion = bf16[12288,3072]{1,0:T(8,128)(2,1)} fusion(f32[12288,3072]{1,0:T(8,128)} %fusion.13, bf16[12288,1024]{1,0:T(8,128)(2,1)} %bitcast.52, bf16[1024,3072]{1,0:T(8,128)(2,1)} %param.14), kind=kOutput, calls=%fused_computation.20 | convolution fusion | flops 77384908800 | bytes 257949696 | tf_op jit(solution)/shard_map/dot_general | solution.py:28
  2270.4 0.0 all-reduce.2.cloned.1.call-update
  2270.5 0.0 copy-start.1
  2270.5 1231.1 %all-reduce.2.cloned.1.call-done = bf16[6,2048,3072]{2,1,0:T(8,128)(2,1)} async-done(((bf16[6,2048,3072]{2,1,0:T(8,128)(2,1)}), bf16[6,2048,3072]{2,1,0:T(8,128)(2,1)}) %all-reduce.2.cloned.1.call-update) | async-done | bytes 75497488 | tf_op jit(solution)/shard_map/psum | solution.py:34
  3501.6 72.9 %fusion.12 = bf16[6,2048,3072]{2,1,0:T(8,128)(2,1)} fusion(bf16[6,2048,3072]{2,1,0:T(8,128)(2,1)} %param.9, bf16[6,2048,3072]{2,1,0:T(8,128)(2,1)} %all-reduce.2.cloned.1.call-done), kind=kLoop, calls=%fused_computation.19 | loop fusion | flops 150994944 | bytes 226492416 | tf_op jit(solution)/shard_map/convert_element_type | solution.py:35
  3574.5 0.0 copy-done.1
  (2 shorter events, 0.0 us)
Async XLA Ops:
  6.5 104.4 %copy-start = (bf16[3072,512]{1,0:T(8,128)(2,1)S(1)}, bf16[3072,512]{1,0:T(8,128)(2,1)}, u32[]{:S(2)}) copy-start(bf16[3072,512]{1,0:T(8,128)(2,1)} %param.13) | copy-start | bytes 9437188
  6.5 3495.0 %all-reduce.2.cloned.1.call-start = ((), (), s32[]{:S(2)}) async-start(), calls=%async_computation | async-start | bytes 150994944 | tf_op jit(solution)/shard_map/psum | solution.py:34
  10.6 50.7 %copy-start.2 = (f32[3072]{0:T(1024)S(1)}, f32[3072]{0:T(1024)}, u32[]{:S(2)}) copy-start(f32[3072]{0:T(1024)} %param.11) | copy-start | bytes 36868
  10.6 50.7 %copy-start.3 = (f32[3072]{0:T(1024)S(1)}, f32[3072]{0:T(1024)}, u32[]{:S(2)}) copy-start(f32[3072]{0:T(1024)} %param.10) | copy-start | bytes 36868
  2270.5 1304.0 %copy-start.1 = (bf16[3072,512]{1,0:T(8,128)(2,1)S(1)}, bf16[3072,512]{1,0:T(8,128)(2,1)}, u32[]{:S(2)}) copy-start(bf16[3072,512]{1,0:T(8,128)(2,1)} %param.13) | copy-start | bytes 9437188
Sparse Core Ops, SparseCore 0:
  2270.6 1230.9 all-reduce.1
where the time goes:
time: 3590 us; the launch traced here: 3580 us
  matrix products  2060 us (57%)
  waiting for transfers between devices  1230 us (34%)
  other arithmetic  177 us (5%)
  local copies, waits for them, and re-layouts  104 us (3%)
    psum x1, waiting for transfers between devices, local(): tot = lax.psum(part, 'tp')  1230 us
    dot_general x1, matrix products, local(): m = jnp.dot(hm, w2, preferred_element_type=jnp.float32)  534 us
    dot_general x1, matrix products, local(): u = jnp.dot(ln, w3, preferred_element_type=jnp.float32)  488 us
    dot_general x1, matrix products, local(): g = jnp.dot(ln, w1, preferred_element_type=jnp.float32)  488 us
    sub x1, matrix products, local(): p = jax.nn.softmax(sc, axis=-1).astype(jnp.bfloat16)  184 us
    dot_general x1, matrix products, local(): jnp.einsum('bhqk,bke->bqhe', p, v, preferred_element_type=jnp.float32)  130 us
    dot_general x1, matrix products, local(): a = jnp.dot(o, wo, preferred_element_type=jnp.float32)  94.6 us
    dot_general x1, matrix products, local(): jnp.dot(ln, wq, preferred_element_type=jnp.float32).astype(jnp.bfloat16)  87.5 us
  transfers between devices with their start and end apart: 1, of which 1 were waited for; matrix products, arithmetic and copies ran while one was open for 0% of the time, Pallas kernels for 0%

commit v1 on v0

v1 whole, which is shorter than its diff:
```python
import functools

import jax
import jax.numpy as jnp
from jax import lax
from jax.experimental import pallas as pl
from jax.experimental.pallas import tpu as pltpu
from jax.sharding import PartitionSpec as P

EPS = 1e-5
LOG2E = 1.4426950408889634
BF = jnp.bfloat16
F32 = jnp.float32
RG = 16
VMEM_LIMIT = 63 * 2**20


def _params(n):
    return pltpu.CompilerParams(dimension_semantics=("arbitrary",) * n, vmem_limit_bytes=VMEM_LIMIT)


def _dot(a, b):
    return jnp.dot(a, b, preferred_element_type=F32)


def _cost(flops, nbytes):
    return pl.CostEstimate(flops=flops, bytes_accessed=nbytes, transcendentals=0)


def _qkv_kernel(x_ref, g_ref, b_ref, wq_ref, wkv_ref, ln_ref, q_ref, kv_ref, *, mc, nc):
    tm = x_ref.shape[0]
    rg = 16
    for r0 in range(0, tm, mc):
        for r in range(r0, r0 + mc, rg):
            xf = x_ref[r:r + rg, :].astype(F32)
            mu = jnp.mean(xf, axis=-1, keepdims=True)
            xc = xf - mu
            var = jnp.mean(xc * xc, axis=-1, keepdims=True)
            ln_ref[r:r + rg, :] = (xc * lax.rsqrt(var + EPS) * g_ref[...] + b_ref[...]).astype(BF)
        a = ln_ref[r0:r0 + mc, :]
        for w_ref, out_ref in ((wq_ref, q_ref), (wkv_ref, kv_ref)):
            for c in range(0, w_ref.shape[1], nc):
                out_ref[r0:r0 + mc, c:c + nc] = _dot(a, w_ref[:, c:c + nc]).astype(BF)


def _qkv(x, gamma, beta, wq, wkv, tm, mc, nc):
    t, d = x.shape
    nq, nkv = wq.shape[1], wkv.shape[1]
    row = lambda i: (i, 0)
    whole = lambda i: (0, 0)
    one = pl.Buffered(1)
    return pl.pallas_call(
        functools.partial(_qkv_kernel, mc=mc, nc=nc),
        grid=(t // tm,),
        in_specs=[pl.BlockSpec((tm, d), row), pl.BlockSpec((1, d), whole), pl.BlockSpec((1, d), whole),
                  pl.BlockSpec((d, nq), whole, pipeline_mode=one), pl.BlockSpec((d, nkv), whole, pipeline_mode=one)],
        out_specs=[pl.BlockSpec((tm, d), row), pl.BlockSpec((tm, nq), row), pl.BlockSpec((tm, nkv), row)],
        out_shape=[jax.ShapeDtypeStruct((t, d), BF), jax.ShapeDtypeStruct((t, nq), BF), jax.ShapeDtypeStruct((t, nkv), BF)],
        compiler_params=_params(1),
        cost_estimate=_cost(2 * t * d * (nq + nkv), 4 * t * d),
        name="qkv",
    )(x, gamma.reshape(1, d), beta.reshape(1, d), wq, wkv)


def _attn_kernel(q_ref, kv_ref, o_ref, *, seq, tq, dh, nh):
    i = pl.program_id(1)
    c2 = LOG2E * dh ** -0.5

    def block(c):
        end = (c + 1) * tq
        lo = end - tq
        row = lax.broadcasted_iota(jnp.int32, (tq, tq), 0)
        col = lax.broadcasted_iota(jnp.int32, (tq, tq), 1)
        for h in range(nh):
            q = q_ref[:, h * dh:(h + 1) * dh]
            s = lax.dot_general(q, kv_ref[:end, :dh], (((1,), (1,)), ((), ())), preferred_element_type=F32)
            sd = jnp.where(col <= row, s[:, lo:], -1e30)
            m = jnp.max(sd, axis=1, keepdims=True)
            if c:
                m = jnp.maximum(m, jnp.max(s[:, :lo], axis=1, keepdims=True))
            mc = m * c2
            p = jnp.exp2(sd * c2 - mc)
            l = jnp.sum(p, axis=1, keepdims=True)
            o = _dot(p.astype(BF), kv_ref[lo:end, dh:])
            if c:
                p = jnp.exp2(s[:, :lo] * c2 - mc)
                l = l + jnp.sum(p, axis=1, keepdims=True)
                o = o + _dot(p.astype(BF), kv_ref[:lo, dh:])
            o_ref[:, h * dh:(h + 1) * dh] = (o * (1.0 / l)).astype(BF)

    for c in range(seq // tq):
        @pl.when(i == c)
        def _(c=c):
            block(c)


def _attn(q, kv, seq, tq):
    t, w = q.shape
    dh = kv.shape[1] // 2
    nh = w // dh
    nq = seq // tq
    return pl.pallas_call(
        functools.partial(_attn_kernel, seq=seq, tq=tq, dh=dh, nh=nh),
        grid=(t // seq, nq),
        in_specs=[pl.BlockSpec((tq, w), lambda b, i: (b * nq + i, 0)), pl.BlockSpec((seq, 2 * dh), lambda b, i: (b, 0))],
        out_specs=pl.BlockSpec((tq, w), lambda b, i: (b * nq + i, 0)),
        out_shape=jax.ShapeDtypeStruct((t, w), BF),
        compiler_params=_params(2),
        cost_estimate=_cost(2 * t * seq * w, 4 * t * w),
        name="attn",
    )(q, kv)


def _mlp_kernel(x_hbm, ln_hbm, o_hbm, w1_hbm, w3_hbm, w2_hbm, wo_hbm, y_hbm,
                ln_v, o_v, h_v, wa, wb, wc, csy, pbuf, rbuf, xbuf, xin,
                wsem, lsem, osem, dsend, drecv, xsend, xrecv, xisem, ylsem, yssem, yrsem, *, nf, nn, tc):
    b, s = pl.program_id(0), pl.program_id(1)
    nb = pl.num_programs(0)
    ns = nf + nn
    np_ = 2 * nn
    tm, d = ln_v.shape
    hr = tm // 2
    me = lax.axis_index("tp")
    core = lax.rem(me, 2)
    other = {"tp": me + 1 - 2 * core}
    across = {"tp": lax.rem(me + 2, 4)}
    mesh_id = pl.DeviceIdType.MESH
    t = b * ns + s
    slot = lax.rem(t, 2)
    yb0 = 2 * np_ * hr

    def w_copies(step, sl):
        w = o_v.shape[1]
        at = pl.ds(sl * d, d)
        col = pl.ds(pl.multiple_of(step * (2 * tc), 2 * tc), 2 * tc)
        out1 = [(w1_hbm.at[:, col], wa.at[at], wsem.at[sl, 0]), (w3_hbm.at[:, col], wb.at[at], wsem.at[sl, 1])]
        col = pl.ds(pl.multiple_of((step - nf) * (2 * tc), 2 * tc), 2 * tc)
        out2 = [(w2_hbm.at[pl.ds(0, d), col], wa.at[at], wsem.at[sl, 0]), (w2_hbm.at[pl.ds(d, d), col], wb.at[at], wsem.at[sl, 1]),
                (wo_hbm.at[:, col], wc.at[pl.ds(sl * w, w)], wsem.at[sl, 2])]
        return out1, out2

    def w_do(step, sl, what):
        one, two = w_copies(step, sl)

        @pl.when(step < nf)
        def _():
            for c in one:
                getattr(pltpu.make_async_copy(*c), what)()

        @pl.when(step >= nf)
        def _():
            for c in two:
                getattr(pltpu.make_async_copy(*c), what)()

    def ln_copy(i):
        return pltpu.make_async_copy(ln_hbm.at[pl.ds(i * tm, tm)], ln_v, lsem)

    def o_copy(i):
        return pltpu.make_async_copy(o_hbm.at[pl.ds(i * tm, tm)], o_v, osem)

    def cs_at(par, i, r=0, n=hr):
        return pl.ds((par * np_ + i) * hr + r, n)

    def half_copy(blk, i):
        return pltpu.make_async_remote_copy(pbuf.at[i, 1 - core], rbuf.at[lax.rem(blk, 2), i], dsend.at[i],
                                            drecv.at[lax.rem(blk, 2), i], device_id=other, device_id_type=mesh_id)

    def sum_copy(blk, i):
        return pltpu.make_async_remote_copy(csy.at[cs_at(lax.rem(blk, 2), i)], xbuf.at[lax.rem(blk, 2), i], xsend.at[i],
                                            xrecv.at[lax.rem(blk, 2), i], device_id=across, device_id_type=mesh_id)

    def rows(k, c):
        blk, i = k // np_, lax.rem(k, np_)
        return (pl.ds(pl.multiple_of(blk * tm + c * hr, hr), hr), pl.ds(pl.multiple_of(i * tc, tc), tc))

    def x_copy(k):
        sl = lax.rem(k, 2)
        return pltpu.make_async_copy(x_hbm.at[rows(k, core)], xin.at[sl], xisem.at[sl])

    def y_rows(k):
        return csy.at[pl.ds(yb0 + lax.rem(k, 2) * hr, hr)]

    def y_local(k):
        return pltpu.make_async_copy(y_rows(k), y_hbm.at[rows(k, core)], ylsem.at[lax.rem(k, 2)])

    def y_remote(k):
        blk, i = k // np_, lax.rem(k, np_)
        return pltpu.make_async_remote_copy(y_rows(k), y_hbm.at[rows(k, core)], yssem.at[lax.rem(k, 2)],
                                            yrsem.at[lax.rem(blk, 2), i], device_id=other, device_id_type=mesh_id)

    def y_arrival(k):
        blk, i = k // np_, lax.rem(k, np_)
        return pltpu.make_async_remote_copy(y_rows(k), y_hbm.at[rows(k, 1 - core)], yssem.at[lax.rem(k, 2)],
                                            yrsem.at[lax.rem(blk, 2), i], device_id=other, device_id_type=mesh_id)

    def cs_wait(blk, i):
        half_copy(blk, i).wait_recv()
        half_copy(blk, i).wait_send()

    def cs_add(par, i):
        for r in range(0, hr, RG):
            at = pl.ds(r, RG)
            csy[cs_at(par, i, r, RG), :] = (pbuf[i, core, at].astype(F32) + rbuf[par, i, at].astype(F32)).astype(BF)

    def y_wait(k):
        blk, i = k // np_, lax.rem(k, np_)
        sum_copy(blk, i).wait_recv()
        sum_copy(blk, i).wait_send()
        x_copy(k).wait()

        @pl.when(k >= 2)
        def _():
            y_local(k - 2).wait()
            y_remote(k - 2).wait_send()

        @pl.when(k >= np_)
        def _():
            y_arrival(k - np_).wait_recv()

    def y_add(par, i, sl):
        for r in range(0, hr, RG):
            at = pl.ds(r, RG)
            both = csy[cs_at(par, i, r, RG), :].astype(F32) + xbuf[par, i, at].astype(F32)
            csy[pl.ds(yb0 + sl * hr + r, RG), :] = (xin[sl, at].astype(F32) + both).astype(BF)

    def y_write(k):
        y_local(k).start()
        y_remote(k).start()

    @pl.when(t == 0)
    def _():
        barrier = pltpu.get_barrier_semaphore()
        for dev in (other, across):
            pl.semaphore_signal(barrier, inc=1, device_id=dev, device_id_type=mesh_id)
        pl.semaphore_wait(barrier, 2)
        w_do(s, slot, "start")
        ln_copy(b).start()
        x_copy(0).start()

    @pl.when(t < nb * ns - 1)
    def _():
        w_do(lax.rem(s + 1, ns), 1 - slot, "start")

    @pl.when(s == 0)
    def _():
        o_copy(b).start()
        ln_copy(b).wait()

    @pl.when(s == nf)
    def _():
        o_copy(b).wait()

        @pl.when(b < nb - 1)
        def _():
            ln_copy(b + 1).start()

    w_do(s, slot, "wait")

    @pl.when(s < nf)
    def _():
        k = np_ * b + s - (np_ + 3)

        @pl.when(b >= 1)
        def _():
            cs_wait(b - 1, s)

        @pl.when(k >= 0)
        def _():
            y_wait(k)

        cs_add(lax.rem(b + 1, 2), s)
        y_add(jnp.where(k >= 0, lax.rem(k // np_, 2), 1), lax.rem(s + 3, np_), jnp.where(k >= 0, lax.rem(k, 2), 1))
        for sub in range(2):
            at, cl = pl.ds(slot * d, d), pl.ds(sub * tc, tc)
            g = _dot(ln_v[...], wa[at, cl])
            u = _dot(ln_v[...], wb[at, cl])
            h_v[:, pl.ds(pl.multiple_of((s * 2 + sub) * tc, tc), tc)] = (g * jax.nn.sigmoid(g) * u).astype(BF)

        @pl.when(b >= 1)
        def _():
            sum_copy(b - 1, s).start()

        @pl.when(k >= 0)
        def _():
            y_write(k)
            x_copy(k + 1).start()

    @pl.when(s >= nf)
    def _():
        p = s - nf

        @pl.when((b == nb - 1) & (p >= 1))
        def _():
            for j in range(2):
                i = 2 * (p - 1) + j
                cs_wait(b, i)
                cs_add(lax.rem(b, 2), i)
                sum_copy(b, i).start()

        for sub in range(2):
            at, cl = pl.ds(slot * d, d), pl.ds(sub * tc, tc)
            w = o_v.shape[1]
            part = (_dot(h_v[:, :d], wa[at, cl]) + _dot(h_v[:, d:], wb[at, cl])
                    + _dot(o_v[...], wc[pl.ds(slot * w, w), cl])).astype(BF)
            for c in range(2):
                pbuf[2 * p + sub, c] = part[c * hr:(c + 1) * hr]
        for sub in range(2):
            half_copy(b, 2 * p + sub).start()

    @pl.when(t == nb * ns - 1)
    def _():
        for i in range(np_ - 2, np_):
            cs_wait(b, i)
            cs_add(lax.rem(b, 2), i)
            sum_copy(b, i).start()

        def finish(k, carry):
            y_wait(k)
            y_add(lax.rem(k // np_, 2), lax.rem(k, np_), lax.rem(k, 2))
            y_write(k)

            @pl.when(k + 1 < np_ * nb)
            def _():
                x_copy(k + 1).start()
            return carry

        last = np_ * nb
        lax.fori_loop(last - np_ - 3, last, finish, 0)
        for k in (last - 2, last - 1):
            y_local(k).wait()
            y_remote(k).wait_send()

        def drain(k, carry):
            y_arrival(k).wait_recv()
            return carry

        lax.fori_loop(last - np_, last, drain, 0)


def _mlp(x, ln, o, w1, w3, w2, wo, tm, tc):
    t, d = x.shape
    f, w = w1.shape[1], o.shape[1]
    nf, nn = f // (2 * tc), d // (2 * tc)
    assert nf == 2 * nn and f == 2 * d
    nb = t // tm
    np_, hr = 2 * nn, tm // 2
    hbm = pl.BlockSpec(memory_space=pltpu.HBM)
    dma = pltpu.SemaphoreType.DMA
    return pl.pallas_call(
        functools.partial(_mlp_kernel, nf=nf, nn=nn, tc=tc),
        grid=(nb, nf + nn),
        in_specs=[hbm] * 7,
        out_specs=hbm,
        out_shape=jax.ShapeDtypeStruct((t, d), BF),
        scratch_shapes=[pltpu.VMEM((tm, d), BF), pltpu.VMEM((tm, w), BF), pltpu.VMEM((tm, f), BF),
                        pltpu.VMEM((2 * d, 2 * tc), BF), pltpu.VMEM((2 * d, 2 * tc), BF), pltpu.VMEM((2 * w, 2 * tc), BF), pltpu.VMEM(((2 * np_ + 2) * hr, tc), BF),
                        pltpu.VMEM((np_, 2, hr, tc), BF), pltpu.VMEM((2, np_, hr, tc), BF), pltpu.VMEM((2, np_, hr, tc), BF),
                        pltpu.VMEM((2, hr, tc), BF),
                        dma((2, 3)), dma(()), dma(()), dma((np_,)), dma((2, np_)), dma((np_,)), dma((2, np_)),
                        dma((2,)), dma((2,)), dma((2,)), dma((2, np_))],
        compiler_params=pltpu.CompilerParams(dimension_semantics=("arbitrary",) * 2, vmem_limit_bytes=VMEM_LIMIT,
                                             collective_id=0, has_side_effects=True),
        cost_estimate=_cost(2 * t * (3 * d * f + d * w), 2 * t * (3 * d + w) + 6 * d * f * nb),
        name="mlp",
    )(x, ln, o, w1, w3, w2, wo)


def solution(mesh):
    def local(x, gamma, beta, wq, wkv, wo, w1, w3, w2):
        b, s, d = x.shape
        t = b * s
        xt = x.reshape(t, d)
        ln, q, kv = _qkv(xt, gamma, beta, wq, wkv, 512, 128, 512)
        o = _attn(q, kv, s, 512)
        return _mlp(xt, ln, o, w1, w3, w2, wo, 512, d // 6).reshape(b, s, d)

    return jax.shard_map(local, mesh=mesh,
                         in_specs=(P('dp', None, None), P(), P(), P(None, 'tp'), P(), P('tp', None),
                                   P(None, 'tp'), P(None, 'tp'), P('tp', None)),
                         out_specs=P('dp', None, None), check_vma=False)
```

time: 3590 us -> 1990 us (0.55)
  matrix products: 2060 us -> 0 us
  Pallas kernels: 0 us -> 1940 us
  waiting for transfers between devices: 1230 us -> 0 us
  other arithmetic: 177 us -> 0 us
  local copies, waits for them, and re-layouts: 104 us -> 49.1 us
    pallas_call x0 -> x3, Pallas kernels: none -> 1940 us  [the longest x1 1690 us: _mlp(): pl.pallas_call(functools.partial(_mlp_kernel, nf=nf, nn=nn, tc=tc), grid=...]
    dot_general x7 -> x0, matrix products: 1870 us -> none  [the longest x1 534 us: local(): m = jnp.dot(hm, w2, preferred_element_type=jnp.float32)]
    psum x1 -> x0, waiting for transfers between devices: 1230 us -> none  [local(): tot = lax.psum(part, 'tp')]
    sub x1 -> x0, matrix products: 184 us -> none  [local(): p = jax.nn.softmax(sc, axis=-1).astype(jnp.bfloat16)]
    convert_element_type x2 -> x0, other arithmetic: 122 us -> none  [the longest x1 72.9 us: local(): return (xf + tot.astype(jnp.float32).reshape(b, s, d)).astype(jnp.bfloat16)]
    reduce_sum x2 -> x0, other arithmetic: 50.6 us -> none  [the longest x1 27.2 us: local(): var = jnp.mean(jnp.square(xf - mu), axis=-1, keepdims=True)]
    reshape x1 -> x0, local copies, waits for them, and re-layouts: 41.2 us -> none  [local(): jnp.dot(ln, wq, preferred_element_type=jnp.float32).astype(jnp.bfloat16)]
    convert_element_type x1 -> x0, local copies, waits for them, and re-layouts: 38.3 us -> none  [local(): jnp.einsum('bhqk,bke->bqhe', p, v, preferred_element_type=jnp.float32)]
  transfers between devices with their start and end apart: 1 -> 0, of which waited for: 1 -> 0; matrix products, arithmetic and copies ran while one was open for 0% -> 0% of each run, Pallas kernels for 0% -> 0%
where the time goes in v1:
time: 1990 us
  Pallas kernels  1940 us (97%)
  local copies, waits for them, and re-layouts  49.1 us (2%)
    pallas_call x1, Pallas kernels, _mlp(): pl.pallas_call(functools.partial(_mlp_kernel, nf=nf, nn=nn, tc=tc), grid=...  1690 us
    pallas_call x1, Pallas kernels, _qkv(): pl.pallas_call(functools.partial(_qkv_kernel, mc=mc, nc=nc), grid=(t // t...  152 us
    pallas_call x1, Pallas kernels, _attn(): pl.pallas_call(functools.partial(_attn_kernel, seq=seq, tq=tq, dh=dh, nh=...  99.9 us
    unnamed x1, local copies, waits for them, and re-layouts  49.1 us

profile of v1, /device:TPU:0, one launch (start us, length us, event | category | flops | bytes accessed | tf_op | source)
XLA Modules:
  0.0 1990.7 jit_solution(6613693509316950821)
XLA Ops:
  0.0 152.3 %qkv.1 = (bf16[12288,3072]{1,0:T(8,128)(2,1)}, bf16[12288,1024]{1,0:T(8,128)(2,1)}, bf16[12288,512]{1,0:T(8,128)(2,1)}) custom-call(bf16[12288,3072]{1,0:T(8,128)(2,1)} %bitcast.x_ref.x_hbm, f32[1,3072]{1,0:T(1,128)} %bitcast.4, f32[1,3072]{1,0:T(1,128)} %bitcast.5, bf16[3072,1024]{1,0:T(8,128)(2,1)} %wq_ref.1, bf16[3072,512]{1,0:T(8,128)(2,1)} %wkv_ref.1), custom_call_target="tpu_custom_call" | custom-call | flops 115964116992 | bytes 150994944 | tf_op jit(solution)/shard_map/qkv/pallas_call | solution.py:52
  152.3 99.9 %attn.1.o_hbm = bf16[12288,1024]{1,0:T(8,128)(2,1)} custom-call(bf16[12288,1024]{1,0:T(8,128)(2,1)} %get-tuple-element.9.q_ref, bf16[12288,512]{1,0:T(8,128)(2,1)} %get-tuple-element.10.kv_ref), custom_call_target="tpu_custom_call" | custom-call | flops 51539607552 | bytes 50331648 | tf_op jit(solution)/shard_map/attn/pallas_call | solution.py:102
  252.3 1689.4 %mlp.1 = bf16[12288,3072]{1,0:T(8,128)(2,1)} custom-call(bf16[12288,3072]{1,0:T(8,128)(2,1)} %bitcast.x_ref.x_hbm, bf16[12288,3072]{1,0:T(8,128)(2,1)} %get-tuple-element.8.ln_hbm, bf16[12288,1024]{1,0:T(8,128)(2,1)} %attn.1.o_hbm, bf16[3072,6144]{1,0:T(8,128)(2,1)} %w1_hbm.1, bf16[3072,6144]{1,0:T(8,128)(2,1)} %w3_hbm.1, bf16[6144,3072]{1,0:T(8,128)(2,1)} %w2_hbm.1, ...), custom_call_target="tpu_custom_call" | custom-call | flops 1468878815232 | bytes 2969567232 | tf_op jit(solution)/shard_map/mlp/pallas_call | solution.py:349
  1941.6 49.1 %copy.11 = bf16[6,2048,3072]{2,1,0:T(8,128)(2,1)} copy(bf16[6,2048,3072]{2,1,0:T(8,128)(2,1)} %bitcast.3) | data formatting | bytes 150994944

commit v2 on v1

v2 whole, which is shorter than its diff:
```python
import functools

import jax
import jax.numpy as jnp
from jax import lax
from jax.experimental import pallas as pl
from jax.experimental.pallas import tpu as pltpu
from jax.sharding import PartitionSpec as P

EPS = 1e-5
LOG2E = 1.4426950408889634
BF = jnp.bfloat16
F32 = jnp.float32
VMEM_LIMIT = 63 * 2**20


def _params(n):
    return pltpu.CompilerParams(dimension_semantics=("arbitrary",) * n, vmem_limit_bytes=VMEM_LIMIT)


def _dot(a, b):
    return jnp.dot(a, b, preferred_element_type=F32)


def _cost(flops, nbytes):
    return pl.CostEstimate(flops=flops, bytes_accessed=nbytes, transcendentals=0)


def _qkv_kernel(x_ref, g_ref, b_ref, wq_ref, wkv_ref, ln_ref, q_ref, kv_ref, *, mc, nc):
    tm = x_ref.shape[0]
    rg = 16
    for r0 in range(0, tm, mc):
        for r in range(r0, r0 + mc, rg):
            xf = x_ref[r:r + rg, :].astype(F32)
            mu = jnp.mean(xf, axis=-1, keepdims=True)
            xc = xf - mu
            var = jnp.mean(xc * xc, axis=-1, keepdims=True)
            ln_ref[r:r + rg, :] = (xc * lax.rsqrt(var + EPS) * g_ref[...] + b_ref[...]).astype(BF)
        a = ln_ref[r0:r0 + mc, :]
        for w_ref, out_ref in ((wq_ref, q_ref), (wkv_ref, kv_ref)):
            for c in range(0, w_ref.shape[1], nc):
                out_ref[r0:r0 + mc, c:c + nc] = _dot(a, w_ref[:, c:c + nc]).astype(BF)


def _qkv(x, gamma, beta, wq, wkv, tm, mc, nc):
    t, d = x.shape
    nq, nkv = wq.shape[1], wkv.shape[1]
    row = lambda i: (i, 0)
    whole = lambda i: (0, 0)
    one = pl.Buffered(1)
    return pl.pallas_call(
        functools.partial(_qkv_kernel, mc=mc, nc=nc),
        grid=(t // tm,),
        in_specs=[pl.BlockSpec((tm, d), row), pl.BlockSpec((1, d), whole), pl.BlockSpec((1, d), whole),
                  pl.BlockSpec((d, nq), whole, pipeline_mode=one), pl.BlockSpec((d, nkv), whole, pipeline_mode=one)],
        out_specs=[pl.BlockSpec((tm, d), row), pl.BlockSpec((tm, nq), row), pl.BlockSpec((tm, nkv), row)],
        out_shape=[jax.ShapeDtypeStruct((t, d), BF), jax.ShapeDtypeStruct((t, nq), BF), jax.ShapeDtypeStruct((t, nkv), BF)],
        compiler_params=_params(1),
        cost_estimate=_cost(2 * t * d * (nq + nkv), 4 * t * d),
        name="qkv",
    )(x, gamma.reshape(1, d), beta.reshape(1, d), wq, wkv)


def _attn_kernel(q_ref, kv_ref, o_ref, *, seq, tq, dh, nh):
    i = pl.program_id(1)
    c2 = LOG2E * dh ** -0.5

    def block(c):
        end = (c + 1) * tq
        lo = end - tq
        row = lax.broadcasted_iota(jnp.int32, (tq, tq), 0)
        col = lax.broadcasted_iota(jnp.int32, (tq, tq), 1)
        for h in range(nh):
            q = q_ref[:, h * dh:(h + 1) * dh]
            s = lax.dot_general(q, kv_ref[:end, :dh], (((1,), (1,)), ((), ())), preferred_element_type=F32)
            sd = jnp.where(col <= row, s[:, lo:], -1e30)
            m = jnp.max(sd, axis=1, keepdims=True)
            if c:
                m = jnp.maximum(m, jnp.max(s[:, :lo], axis=1, keepdims=True))
            mc = m * c2
            p = jnp.exp2(sd * c2 - mc)
            l = jnp.sum(p, axis=1, keepdims=True)
            o = _dot(p.astype(BF), kv_ref[lo:end, dh:])
            if c:
                p = jnp.exp2(s[:, :lo] * c2 - mc)
                l = l + jnp.sum(p, axis=1, keepdims=True)
                o = o + _dot(p.astype(BF), kv_ref[:lo, dh:])
            o_ref[:, h * dh:(h + 1) * dh] = (o * (1.0 / l)).astype(BF)

    for c in range(seq // tq):
        @pl.when(i == c)
        def _(c=c):
            block(c)


def _attn(q, kv, seq, tq):
    t, w = q.shape
    dh = kv.shape[1] // 2
    nh = w // dh
    nq = seq // tq
    return pl.pallas_call(
        functools.partial(_attn_kernel, seq=seq, tq=tq, dh=dh, nh=nh),
        grid=(t // seq, nq),
        in_specs=[pl.BlockSpec((tq, w), lambda b, i: (b * nq + i, 0)), pl.BlockSpec((seq, 2 * dh), lambda b, i: (b, 0))],
        out_specs=pl.BlockSpec((tq, w), lambda b, i: (b * nq + i, 0)),
        out_shape=jax.ShapeDtypeStruct((t, w), BF),
        compiler_params=_params(2),
        cost_estimate=_cost(2 * t * seq * w, 4 * t * w),
        name="attn",
    )(q, kv)


SLOTS = 4
RG = 16


def _mlp_kernel(x_hbm, ln_hbm, o_hbm, w1_hbm, w3_hbm, w2_hbm, wo_hbm, y_hbm,
                ln_v, o_v, h_v, wa, wb, wc, csy, pbuf, rbuf, xbuf, xin,
                wsem, lsem, osem, dsend, drecv, xsend, xrecv, xisem, ylsem, yssem, yrsem, *, nf, nn, uf, un):
    b, s = pl.program_id(0), pl.program_id(1)
    nb = pl.num_programs(0)
    sf = nf // uf
    last_step = sf + nn // un - 1
    tm, d = ln_v.shape
    w = o_v.shape[1]
    tc = wa.shape[1]
    hr = tm // 2
    me = lax.axis_index("tp")
    core = lax.rem(me, 2)
    other = {"tp": me + 1 - 2 * core}
    across = {"tp": lax.rem(me + 2, 4)}
    mesh_id = pl.DeviceIdType.MESH
    ncol = nf + nn
    yb0 = 2 * nn * hr

    def w_copies(g, j, kind):
        sl = lax.rem(g, SLOTS)
        at = pl.ds(sl * d, d)
        if kind == 0:
            col = pl.ds(pl.multiple_of(j * tc, tc), tc)
            todo = [(w1_hbm.at[:, col], wa.at[at]), (w3_hbm.at[:, col], wb.at[at])]
        else:
            col = pl.ds(pl.multiple_of((j - nf) * tc, tc), tc)
            todo = [(w2_hbm.at[pl.ds(0, d), col], wa.at[at]), (w2_hbm.at[pl.ds(d, d), col], wb.at[at]),
                    (wo_hbm.at[:, col], wc.at[pl.ds(sl * w, w)])]
        return [pltpu.make_async_copy(src, dst, wsem.at[sl, i]) for i, (src, dst) in enumerate(todo)]

    def w_wait(g, j, kind):
        for c in w_copies(g, j, kind):
            c.wait()

    def w_start(g):
        j = lax.rem(g, ncol)
        for kind in range(2):
            @pl.when((g < nb * ncol) & ((j < nf) if kind == 0 else (j >= nf)))
            def _(kind=kind):
                for c in w_copies(g, j, kind):
                    c.start()

    def ln_copy(i):
        return pltpu.make_async_copy(ln_hbm.at[pl.ds(i * tm, tm)], ln_v, lsem)

    def o_copy(i):
        return pltpu.make_async_copy(o_hbm.at[pl.ds(i * tm, tm)], o_v, osem)

    def cs_at(par, i, r=0, n=hr):
        return pl.ds((par * nn + i) * hr + r, n)

    def half_copy(blk, i):
        return pltpu.make_async_remote_copy(pbuf.at[i, 1 - core], rbuf.at[lax.rem(blk, 2), i], dsend.at[i],
                                            drecv.at[lax.rem(blk, 2), i], device_id=other, device_id_type=mesh_id)

    def sum_copy(blk, i):
        return pltpu.make_async_remote_copy(csy.at[cs_at(lax.rem(blk, 2), i)], xbuf.at[lax.rem(blk, 2), i], xsend.at[i],
                                            xrecv.at[lax.rem(blk, 2), i], device_id=across, device_id_type=mesh_id)

    def rows(k, c):
        blk, i = k // nn, lax.rem(k, nn)
        return (pl.ds(pl.multiple_of(blk * tm + c * hr, hr), hr), pl.ds(pl.multiple_of(i * tc, tc), tc))

    def x_copy(k):
        sl = lax.rem(k, 2)
        return pltpu.make_async_copy(x_hbm.at[rows(k, core)], xin.at[sl], xisem.at[sl])

    def y_rows(k):
        return csy.at[pl.ds(yb0 + lax.rem(k, 2) * hr, hr)]

    def y_local(k):
        return pltpu.make_async_copy(y_rows(k), y_hbm.at[rows(k, core)], ylsem.at[lax.rem(k, 2)])

    def y_remote(k, c):
        blk, i = k // nn, lax.rem(k, nn)
        return pltpu.make_async_remote_copy(y_rows(k), y_hbm.at[rows(k, c)], yssem.at[lax.rem(k, 2)],
                                            yrsem.at[lax.rem(blk, 2), i], device_id=other, device_id_type=mesh_id)

    def cs_wait(blk, i):
        half_copy(blk, i).wait_recv()
        half_copy(blk, i).wait_send()

    def cs_add(par, i):
        for r in range(0, hr, RG):
            at = pl.ds(r, RG)
            csy[cs_at(par, i, r, RG), :] = (pbuf[i, core, at].astype(F32) + rbuf[par, i, at].astype(F32)).astype(BF)

    def y_wait(k):
        blk, i = k // nn, lax.rem(k, nn)
        sum_copy(blk, i).wait_recv()
        sum_copy(blk, i).wait_send()
        x_copy(k).wait()

        @pl.when(k >= 2)
        def _():
            y_local(k - 2).wait()
            y_remote(k - 2, core).wait_send()

        @pl.when(k >= nn)
        def _():
            y_remote(k - nn, 1 - core).wait_recv()

    def y_add(par, i, sl):
        for r in range(0, hr, RG):
            at = pl.ds(r, RG)
            both = csy[cs_at(par, i, r, RG), :].astype(F32) + xbuf[par, i, at].astype(F32)
            csy[pl.ds(yb0 + sl * hr + r, RG), :] = (xin[sl, at].astype(F32) + both).astype(BF)

    def y_write(k):
        y_local(k).start()
        y_remote(k, core).start()

        @pl.when(k + 1 < nn * nb)
        def _():
            x_copy(k + 1).start()

    @pl.when((b == 0) & (s == 0))
    def _():
        barrier = pltpu.get_barrier_semaphore()
        for dev in (other, across):
            pl.semaphore_signal(barrier, inc=1, device_id=dev, device_id_type=mesh_id)
        pl.semaphore_wait(barrier, 2)
        for g in range(SLOTS - 1):
            w_start(jnp.int32(g))
        ln_copy(b).start()
        x_copy(0).start()

    @pl.when(s == 0)
    def _():
        o_copy(b).start()
        ln_copy(b).wait()

    @pl.when(s == sf)
    def _():
        o_copy(b).wait()

        @pl.when(b < nb - 1)
        def _():
            ln_copy(b + 1).start()

    k = nn * b + s - nn - 2

    @pl.when(b >= 1)
    def _():
        cs_wait(b - 1, s)

    @pl.when(k >= 0)
    def _():
        y_wait(k)

    def sums():
        cs_add(lax.rem(b + 1, 2), s)
        y_add(jnp.where(k >= 0, lax.rem(k // nn, 2), 1), lax.rem(s + nn - 2, nn), jnp.where(k >= 0, lax.rem(k, 2), 1))

    def early_sums(items):
        for i in items:
            cs_wait(b, i)
            cs_add(lax.rem(b, 2), i)
            sum_copy(b, i).start()

    @pl.when(s < sf)
    def _():
        j0 = s * uf
        g0 = b * ncol + j0
        for u in range(uf):
            w_wait(g0 + u, j0 + u, 0)
        sums()
        for u in range(uf):
            w_start(g0 + u + SLOTS - 1)
            at = pl.ds(lax.rem(g0 + u, SLOTS) * d, d)
            gate = _dot(ln_v[...], wa[at, :])
            up = _dot(ln_v[...], wb[at, :])
            h_v[:, pl.ds(pl.multiple_of((j0 + u) * tc, tc), tc)] = (gate * jax.nn.sigmoid(gate) * up).astype(BF)

    @pl.when(s >= sf)
    def _():
        n0 = (s - sf) * un
        g0 = b * ncol + nf + n0

        @pl.when((b == nb - 1) & (s == last_step))
        def _():
            early_sums(range(nn - un))

        for u in range(un):
            w_wait(g0 + u, nf + n0 + u, 1)
        sums()
        for u in range(un):
            w_start(g0 + u + SLOTS - 1)
            sl = lax.rem(g0 + u, SLOTS)
            at = pl.ds(sl * d, d)
            part = (_dot(h_v[:, :d], wa[at, :]) + _dot(h_v[:, d:], wb[at, :])
                    + _dot(o_v[...], wc[pl.ds(sl * w, w), :])).astype(BF)
            for c in range(2):
                pbuf[n0 + u, c] = part[c * hr:(c + 1) * hr]
        for u in range(un):
            half_copy(b, n0 + u).start()

    @pl.when(b >= 1)
    def _():
        sum_copy(b - 1, s).start()

    @pl.when(k >= 0)
    def _():
        y_write(k)

    @pl.when((b == nb - 1) & (s == last_step))
    def _():
        last = nn * nb

        def finish(k, carry):
            y_wait(k)
            y_add(lax.rem(k // nn, 2), lax.rem(k, nn), lax.rem(k, 2))
            y_write(k)
            return carry

        early_sums(range(nn - un, nn))
        lax.fori_loop(last - nn - 2, last, finish, 0)
        for k in (last - 2, last - 1):
            y_local(k).wait()
            y_remote(k, core).wait_send()

        def drain(k, carry):
            y_remote(k, 1 - core).wait_recv()
            return carry

        lax.fori_loop(last - nn, last, drain, 0)


def _mlp(x, ln, o, w1, w3, w2, wo, tm, tc, uf, un):
    t, d = x.shape
    f, w = w1.shape[1], o.shape[1]
    nf, nn = f // tc, d // tc
    nb = t // tm
    hr = tm // 2
    assert f == 2 * d and nf // uf + nn // un == nn and nf % uf == 0 and nn % un == 0
    hbm = pl.BlockSpec(memory_space=pltpu.HBM)
    dma = pltpu.SemaphoreType.DMA
    return pl.pallas_call(
        functools.partial(_mlp_kernel, nf=nf, nn=nn, uf=uf, un=un),
        grid=(nb, nf // uf + nn // un),
        in_specs=[hbm] * 7,
        out_specs=hbm,
        out_shape=jax.ShapeDtypeStruct((t, d), BF),
        scratch_shapes=[pltpu.VMEM((tm, d), BF), pltpu.VMEM((tm, w), BF), pltpu.VMEM((tm, f), BF),
                        pltpu.VMEM((SLOTS * d, tc), BF), pltpu.VMEM((SLOTS * d, tc), BF), pltpu.VMEM((SLOTS * w, tc), BF),
                        pltpu.VMEM(((2 * nn + 2) * hr, tc), BF),
                        pltpu.VMEM((nn, 2, hr, tc), BF), pltpu.VMEM((2, nn, hr, tc), BF), pltpu.VMEM((2, nn, hr, tc), BF),
                        pltpu.VMEM((2, hr, tc), BF),
                        dma((SLOTS, 3)), dma(()), dma(()), dma((nn,)), dma((2, nn)), dma((nn,)), dma((2, nn)),
                        dma((2,)), dma((2,)), dma((2,)), dma((2, nn))],
        compiler_params=pltpu.CompilerParams(dimension_semantics=("arbitrary",) * 2, vmem_limit_bytes=VMEM_LIMIT,
                                             collective_id=0, has_side_effects=True),
        cost_estimate=_cost(2 * t * (3 * d * f + d * w), 2 * t * (3 * d + w) + 6 * d * f * nb),
        name="mlp",
    )(x, ln, o, w1, w3, w2, wo)


def solution(mesh):
    def local(x, gamma, beta, wq, wkv, wo, w1, w3, w2):
        b, s, d = x.shape
        t = b * s
        xt = x.reshape(t, d)
        ln, q, kv = _qkv(xt, gamma, beta, wq, wkv, 512, 128, 512)
        o = _attn(q, kv, s, 512)
        return _mlp(xt, ln, o, w1, w3, w2, wo, 512, d // 6, 3, 3).reshape(b, s, d)

    return jax.shard_map(local, mesh=mesh,
                         in_specs=(P('dp', None, None), P(), P(), P(None, 'tp'), P(), P('tp', None),
                                   P(None, 'tp'), P(None, 'tp'), P('tp', None)),
                         out_specs=P('dp', None, None), check_vma=False)
```

time: 1990 us -> 2030 us (1.020)
  Pallas kernels: 1940 us -> 1970 us
where the time goes in v2:
time: 2030 us; the launch traced here: 2020 us
  Pallas kernels  1970 us (97%)
  local copies, waits for them, and re-layouts  49.1 us (2%)
    pallas_call x1, Pallas kernels, _mlp(): pl.pallas_call(functools.partial(_mlp_kernel, nf=nf, nn=nn, uf=uf, un=un)...  1710 us
    pallas_call x1, Pallas kernels, _qkv(): pl.pallas_call(functools.partial(_qkv_kernel, mc=mc, nc=nc), grid=(t // t...  152 us
    pallas_call x1, Pallas kernels, _attn(): pl.pallas_call(functools.partial(_attn_kernel, seq=seq, tq=tq, dh=dh, nh=...  110 us
    unnamed x1, local copies, waits for them, and re-layouts  49.1 us

profile of v2, /device:TPU:0, one launch (start us, length us, event | category | flops | bytes accessed | tf_op | source)
XLA Modules:
  0.0 2017.9 jit_solution(9672914619336132341)
XLA Ops:
  0.0 152.4 %qkv.1 = (bf16[12288,3072]{1,0:T(8,128)(2,1)}, bf16[12288,1024]{1,0:T(8,128)(2,1)}, bf16[12288,512]{1,0:T(8,128)(2,1)}) custom-call(bf16[12288,3072]{1,0:T(8,128)(2,1)} %bitcast.x_ref.x_hbm, f32[1,3072]{1,0:T(1,128)} %bitcast.4, f32[1,3072]{1,0:T(1,128)} %bitcast.5, bf16[3072,1024]{1,0:T(8,128)(2,1)} %wq_ref.1, bf16[3072,512]{1,0:T(8,128)(2,1)} %wkv_ref.1), custom_call_target="tpu_custom_call" | custom-call | flops 115964116992 | bytes 150994944 | tf_op jit(solution)/shard_map/qkv/pallas_call | solution.py:51
  152.4 109.8 %attn.1.o_hbm = bf16[12288,1024]{1,0:T(8,128)(2,1)} custom-call(bf16[12288,1024]{1,0:T(8,128)(2,1)} %get-tuple-element.9.q_ref, bf16[12288,512]{1,0:T(8,128)(2,1)} %get-tuple-element.10.kv_ref), custom_call_target="tpu_custom_call" | custom-call | flops 51539607552 | bytes 50331648 | tf_op jit(solution)/shard_map/attn/pallas_call | solution.py:101
  262.2 1706.7 %mlp.1 = bf16[12288,3072]{1,0:T(8,128)(2,1)} custom-call(bf16[12288,3072]{1,0:T(8,128)(2,1)} %bitcast.x_ref.x_hbm, bf16[12288,3072]{1,0:T(8,128)(2,1)} %get-tuple-element.8.ln_hbm, bf16[12288,1024]{1,0:T(8,128)(2,1)} %attn.1.o_hbm, bf16[3072,6144]{1,0:T(8,128)(2,1)} %w1_hbm.1, bf16[3072,6144]{1,0:T(8,128)(2,1)} %w3_hbm.1, bf16[6144,3072]{1,0:T(8,128)(2,1)} %w2_hbm.1, ...), custom_call_target="tpu_custom_call" | custom-call | flops 1468878815232 | bytes 2969567232 | tf_op jit(solution)/shard_map/mlp/pallas_call | solution.py:355
  1968.8 49.1 %copy.11 = bf16[6,2048,3072]{2,1,0:T(8,128)(2,1)} copy(bf16[6,2048,3072]{2,1,0:T(8,128)(2,1)} %bitcast.3) | data formatting | bytes 150994944

commit v3 on v2

--- a/solution.py
+++ b/solution.py
@@ -11,7 +11,7 @@
 LOG2E = 1.4426950408889634
 BF = jnp.bfloat16
 F32 = jnp.float32
-VMEM_LIMIT = 63 * 2**20
+VMEM_LIMIT = 67043328
 
 
 def _params(n):
@@ -110,28 +110,28 @@
     )(q, kv)
 
 
-SLOTS = 4
-RG = 16
+SLOTS = 3
+RG = 32
 
 
 def _mlp_kernel(x_hbm, ln_hbm, o_hbm, w1_hbm, w3_hbm, w2_hbm, wo_hbm, y_hbm,
-                ln_v, o_v, h_v, wa, wb, wc, csy, pbuf, rbuf, xbuf, xin,
-                wsem, lsem, osem, dsend, drecv, xsend, xrecv, xisem, ylsem, yssem, yrsem, *, nf, nn, uf, un):
+                ln_v, o_v, h_v, gate_v, wa, wb, wc, csum, yrow, pieces, rbuf, xbuf, xin,
+                wsem, lsem, osem, dsend, drecv, xsend, xrecv, xisem, ylsem, yssem, yrsem, rfree, xfree, *, nf, nn):
     b, s = pl.program_id(0), pl.program_id(1)
     nb = pl.num_programs(0)
-    sf = nf // uf
-    last_step = sf + nn // un - 1
+    sf, sn = nf // 2, nn // 2
+    last_step = sf + sn - 1
     tm, d = ln_v.shape
     w = o_v.shape[1]
     tc = wa.shape[1]
     hr = tm // 2
+    lag = nn // 2
     me = lax.axis_index("tp")
     core = lax.rem(me, 2)
     other = {"tp": me + 1 - 2 * core}
     across = {"tp": lax.rem(me + 2, 4)}
     mesh_id = pl.DeviceIdType.MESH
     ncol = nf + nn
-    yb0 = 2 * nn * hr
 
     def w_copies(g, j, kind):
         sl = lax.rem(g, SLOTS)
@@ -163,73 +163,108 @@
     def o_copy(i):
         return pltpu.make_async_copy(o_hbm.at[pl.ds(i * tm, tm)], o_v, osem)
 
-    def cs_at(par, i, r=0, n=hr):
-        return pl.ds((par * nn + i) * hr + r, n)
-
-    def half_copy(blk, i):
-        return pltpu.make_async_remote_copy(pbuf.at[i, 1 - core], rbuf.at[lax.rem(blk, 2), i], dsend.at[i],
-                                            drecv.at[lax.rem(blk, 2), i], device_id=other, device_id_type=mesh_id)
-
-    def sum_copy(blk, i):
-        return pltpu.make_async_remote_copy(csy.at[cs_at(lax.rem(blk, 2), i)], xbuf.at[lax.rem(blk, 2), i], xsend.at[i],
-                                            xrecv.at[lax.rem(blk, 2), i], device_id=across, device_id_type=mesh_id)
+    def half_copy(i):
+        return pltpu.make_async_remote_copy(pieces.at[nn + lax.rem(i, 2)], rbuf.at[i], dsend.at[i], drecv.at[i],
+                                            device_id=other, device_id_type=mesh_id)
+
+    def sum_copy(i):
+        return pltpu.make_async_remote_copy(csum.at[i], xbuf.at[i], xsend.at[i], xrecv.at[i],
+                                            device_id=across, device_id_type=mesh_id)
 
     def rows(k, c):
         blk, i = k // nn, lax.rem(k, nn)
         return (pl.ds(pl.multiple_of(blk * tm + c * hr, hr), hr), pl.ds(pl.multiple_of(i * tc, tc), tc))
 
     def x_copy(k):
-        sl = lax.rem(k, 2)
-        return pltpu.make_async_copy(x_hbm.at[rows(k, core)], xin.at[sl], xisem.at[sl])
-
-    def y_rows(k):
-        return csy.at[pl.ds(yb0 + lax.rem(k, 2) * hr, hr)]
+        return pltpu.make_async_copy(x_hbm.at[rows(k, core)], xin.at[0], xisem)
 
     def y_local(k):
-        return pltpu.make_async_copy(y_rows(k), y_hbm.at[rows(k, core)], ylsem.at[lax.rem(k, 2)])
+        return pltpu.make_async_copy(yrow.at[0], y_hbm.at[rows(k, core)], ylsem)
 
     def y_remote(k, c):
-        blk, i = k // nn, lax.rem(k, nn)
-        return pltpu.make_async_remote_copy(y_rows(k), y_hbm.at[rows(k, c)], yssem.at[lax.rem(k, 2)],
-                                            yrsem.at[lax.rem(blk, 2), i], device_id=other, device_id_type=mesh_id)
-
-    def cs_wait(blk, i):
-        half_copy(blk, i).wait_recv()
-        half_copy(blk, i).wait_send()
-
-    def cs_add(par, i):
-        for r in range(0, hr, RG):
-            at = pl.ds(r, RG)
-            csy[cs_at(par, i, r, RG), :] = (pbuf[i, core, at].astype(F32) + rbuf[par, i, at].astype(F32)).astype(BF)
+        return pltpu.make_async_remote_copy(yrow.at[0], y_hbm.at[rows(k, c)], yssem,
+                                            yrsem.at[lax.rem(k // nn, 2), lax.rem(k, nn)], device_id=other, device_id_type=mesh_id)
+
+    def half_start(blk, i):
+        @pl.when(blk >= 1)
+        def _():
+            pl.semaphore_wait(rfree.at[i], 1)
+        half_copy(i).start()
+
+    def cs_wait(i):
+        half_copy(i).wait_recv()
+
+        @pl.when(i >= nn - 2)
+        def _():
+            half_copy(i).wait_send()
+
+    def groups(body, rolled):
+        if rolled:
+            @pl.loop(0, hr // RG)
+            def _(r):
+                body(pl.ds(pl.multiple_of(r * RG, RG), RG))
+        else:
+            for r in range(0, hr, RG):
+                body(pl.ds(r, RG))
+
+    def cs_add(i, r_at, rolled=False):
+        def body(at):
+            csum[i, at] = (pieces[i, at].astype(F32) + rbuf[r_at, at].astype(F32)).astype(BF)
+
+        groups(body, rolled)
+
+    def cs_send(blk, i):
+        @pl.when(blk < nb - 1)
+        def _():
+            pl.semaphore_signal(rfree.at[i], inc=1, device_id=other, device_id_type=mesh_id)
+
+        @pl.when(blk >= 1)
+        def _():
+            pl.semaphore_wait(xfree.at[i], 1)
+        sum_copy(i).start()
 
     def y_wait(k):
-        blk, i = k // nn, lax.rem(k, nn)
-        sum_copy(blk, i).wait_recv()
-        sum_copy(blk, i).wait_send()
+        i = lax.rem(k, nn)
+        sum_copy(i).wait_recv()
+        sum_copy(i).wait_send()
         x_copy(k).wait()
 
-        @pl.when(k >= 2)
-        def _():
-            y_local(k - 2).wait()
-            y_remote(k - 2, core).wait_send()
+        @pl.when(k >= 1)
+        def _():
+            y_local(k - 1).wait()
+            y_remote(k - 1, core).wait_send()
 
         @pl.when(k >= nn)
         def _():
             y_remote(k - nn, 1 - core).wait_recv()
 
-    def y_add(par, i, sl):
-        for r in range(0, hr, RG):
-            at = pl.ds(r, RG)
-            both = csy[cs_at(par, i, r, RG), :].astype(F32) + xbuf[par, i, at].astype(F32)
-            csy[pl.ds(yb0 + sl * hr + r, RG), :] = (xin[sl, at].astype(F32) + both).astype(BF)
+    def y_add(i, x_at, rolled=False):
+        def body(at):
+            both = csum[i, at].astype(F32) + xbuf[x_at, at].astype(F32)
+            yrow[0, at] = (xin[0, at].astype(F32) + both).astype(BF)
+
+        groups(body, rolled)
 
     def y_write(k):
+        @pl.when(k < nn * (nb - 1))
+        def _():
+            pl.semaphore_signal(xfree.at[lax.rem(k, nn)], inc=1, device_id=across, device_id_type=mesh_id)
         y_local(k).start()
         y_remote(k, core).start()
 
+    def y_all(k):
+        y_wait(k)
+        y_add(lax.rem(k, nn), lax.rem(k, nn), rolled=True)
+        y_write(k)
+
         @pl.when(k + 1 < nn * nb)
         def _():
             x_copy(k + 1).start()
+
+    def cs_all(i):
+        cs_wait(i)
+        cs_add(i, i, rolled=True)
+        cs_send(b, i)
 
     @pl.when((b == 0) & (s == 0))
     def _():
@@ -240,7 +275,6 @@
         for g in range(SLOTS - 1):
             w_start(jnp.int32(g))
         ln_copy(b).start()
-        x_copy(0).start()
 
     @pl.when(s == 0)
     def _():
@@ -255,86 +289,96 @@
         def _():
             ln_copy(b + 1).start()
 
-    k = nn * b + s - nn - 2
-
-    @pl.when(b >= 1)
-    def _():
-        cs_wait(b - 1, s)
-
-    @pl.when(k >= 0)
-    def _():
-        y_wait(k)
-
-    def sums():
-        cs_add(lax.rem(b + 1, 2), s)
-        y_add(jnp.where(k >= 0, lax.rem(k // nn, 2), 1), lax.rem(s + nn - 2, nn), jnp.where(k >= 0, lax.rem(k, 2), 1))
-
-    def early_sums(items):
-        for i in items:
-            cs_wait(b, i)
-            cs_add(lax.rem(b, 2), i)
-            sum_copy(b, i).start()
-
     @pl.when(s < sf)
     def _():
-        j0 = s * uf
+        j0 = 2 * s
         g0 = b * ncol + j0
-        for u in range(uf):
+        k = nn * b + s - nn - lag
+
+        @pl.when(b >= 1)
+        def _():
+            cs_wait(s)
+
+        @pl.when(k >= 0)
+        def _():
+            y_wait(k)
+
+        for u in range(2):
             w_wait(g0 + u, j0 + u, 0)
-        sums()
-        for u in range(uf):
+        cs_add(s, jnp.where(b >= 1, s, nn))
+        i = lax.rem(s + nn - lag, nn)
+        y_add(i, jnp.where(k >= 0, i, nn))
+        for u in range(2):
             w_start(g0 + u + SLOTS - 1)
             at = pl.ds(lax.rem(g0 + u, SLOTS) * d, d)
-            gate = _dot(ln_v[...], wa[at, :])
+            gate_v[...] = _dot(ln_v[...], wa[at, :])
             up = _dot(ln_v[...], wb[at, :])
+            gate = gate_v[...]
             h_v[:, pl.ds(pl.multiple_of((j0 + u) * tc, tc), tc)] = (gate * jax.nn.sigmoid(gate) * up).astype(BF)
 
+        @pl.when(b >= 1)
+        def _():
+            cs_send(b - 1, s)
+
+        @pl.when(k >= 0)
+        def _():
+            y_write(k)
+
+        @pl.when(k >= -1)
+        def _():
+            x_copy(k + 1).start()
+
     @pl.when(s >= sf)
     def _():
-        n0 = (s - sf) * un
+        n0 = 2 * (s - sf)
         g0 = b * ncol + nf + n0
 
-        @pl.when((b == nb - 1) & (s == last_step))
-        def _():
-            early_sums(range(nn - un))
-
-        for u in range(un):
+        @pl.when((b == nb - 1) & (s > sf))
+        def _():
+            def old(k, carry):
+                y_all(k)
+                return carry
+
+            first = nn * (b - 1) + nn - lag
+            lax.fori_loop(first + (s - sf - 1) * (lag - 1), jnp.minimum(first + (s - sf) * (lag - 1), nn * b), old, 0)
+
+            @pl.loop(n0 - 2, n0)
+            def _(i):
+                cs_all(i)
+
+        @pl.when(s > sf)
+        def _():
+            for u in range(2):
+                half_copy(n0 - 2 + u).wait_send()
+
+        for u in range(2):
             w_wait(g0 + u, nf + n0 + u, 1)
-        sums()
-        for u in range(un):
+        for u in range(2):
             w_start(g0 + u + SLOTS - 1)
             sl = lax.rem(g0 + u, SLOTS)
             at = pl.ds(sl * d, d)
             part = (_dot(h_v[:, :d], wa[at, :]) + _dot(h_v[:, d:], wb[at, :])
                     + _dot(o_v[...], wc[pl.ds(sl * w, w), :])).astype(BF)
             for c in range(2):
-                pbuf[n0 + u, c] = part[c * hr:(c + 1) * hr]
-        for u in range(un):
-            half_copy(b, n0 + u).start()
-
-    @pl.when(b >= 1)
-    def _():
-        sum_copy(b - 1, s).start()
-
-    @pl.when(k >= 0)
-    def _():
-        y_write(k)
+                pieces[jnp.where(core == c, n0 + u, nn + u)] = part[c * hr:(c + 1) * hr]
+        for u in range(2):
+            half_start(b, n0 + u)
 
     @pl.when((b == nb - 1) & (s == last_step))
     def _():
         last = nn * nb
 
+        @pl.loop(nn - 2, nn)
+        def _(i):
+            cs_all(i)
+
         def finish(k, carry):
-            y_wait(k)
-            y_add(lax.rem(k // nn, 2), lax.rem(k, nn), lax.rem(k, 2))
-            y_write(k)
+            y_all(k)
             return carry
 
-        early_sums(range(nn - un, nn))
-        lax.fori_loop(last - nn - 2, last, finish, 0)
-        for k in (last - 2, last - 1):
-            y_local(k).wait()
-            y_remote(k, core).wait_send()
+        lax.fori_loop(last - nn, last, finish, 0)
+        y_local(last - 1).wait()
+        y_remote(last - 1, core).wait_send()
 
         def drain(k, carry):
             y_remote(k, 1 - core).wait_recv()
@@ -343,28 +387,28 @@
         lax.fori_loop(last - nn, last, drain, 0)
 
 
-def _mlp(x, ln, o, w1, w3, w2, wo, tm, tc, uf, un):
+def _mlp(x, ln, o, w1, w3, w2, wo, tm, tc):
     t, d = x.shape
     f, w = w1.shape[1], o.shape[1]
     nf, nn = f // tc, d // tc
     nb = t // tm
     hr = tm // 2
-    assert f == 2 * d and nf // uf + nn // un == nn and nf % uf == 0 and nn % un == 0
+    assert f == 2 * d and nn == 6
     hbm = pl.BlockSpec(memory_space=pltpu.HBM)
     dma = pltpu.SemaphoreType.DMA
+    half = lambda n: pltpu.VMEM((n, hr, tc), BF)
     return pl.pallas_call(
-        functools.partial(_mlp_kernel, nf=nf, nn=nn, uf=uf, un=un),
-        grid=(nb, nf // uf + nn // un),
+        functools.partial(_mlp_kernel, nf=nf, nn=nn),
+        grid=(nb, (nf + nn) // 2),
         in_specs=[hbm] * 7,
         out_specs=hbm,
         out_shape=jax.ShapeDtypeStruct((t, d), BF),
-        scratch_shapes=[pltpu.VMEM((tm, d), BF), pltpu.VMEM((tm, w), BF), pltpu.VMEM((tm, f), BF),
+        scratch_shapes=[pltpu.VMEM((tm, d), BF), pltpu.VMEM((tm, w), BF), pltpu.VMEM((tm, f), BF), pltpu.VMEM((tm, tc), F32),
                         pltpu.VMEM((SLOTS * d, tc), BF), pltpu.VMEM((SLOTS * d, tc), BF), pltpu.VMEM((SLOTS * w, tc), BF),
-                        pltpu.VMEM(((2 * nn + 2) * hr, tc), BF),
-                        pltpu.VMEM((nn, 2, hr, tc), BF), pltpu.VMEM((2, nn, hr, tc), BF), pltpu.VMEM((2, nn, hr, tc), BF),
-                        pltpu.VMEM((2, hr, tc), BF),
-                        dma((SLOTS, 3)), dma(()), dma(()), dma((nn,)), dma((2, nn)), dma((nn,)), dma((2, nn)),
-                        dma((2,)), dma((2,)), dma((2,)), dma((2, nn))],
+                        half(nn), half(1), half(nn + 2), half(nn + 1), half(nn + 1), half(1),
+                        dma((SLOTS, 3)), dma(()), dma(()), dma((nn,)), dma((nn,)), dma((nn,)), dma((nn,)),
+                        dma(()), dma(()), dma(()), dma((2, nn)),
+                        pltpu.SemaphoreType.REGULAR((nn,)), pltpu.SemaphoreType.REGULAR((nn,))],
         compiler_params=pltpu.CompilerParams(dimension_semantics=("arbitrary",) * 2, vmem_limit_bytes=VMEM_LIMIT,
                                              collective_id=0, has_side_effects=True),
         cost_estimate=_cost(2 * t * (3 * d * f + d * w), 2 * t * (3 * d + w) + 6 * d * f * nb),
@@ -377,9 +421,9 @@
         b, s, d = x.shape
         t = b * s
         xt = x.reshape(t, d)
-        ln, q, kv = _qkv(xt, gamma, beta, wq, wkv, 512, 128, 512)
+        ln, q, kv = _qkv(xt, gamma, beta, wq, wkv, 384, 128, 512)
         o = _attn(q, kv, s, 512)
-        return _mlp(xt, ln, o, w1, w3, w2, wo, 512, d // 6, 3, 3).reshape(b, s, d)
+        return _mlp(xt, ln, o, w1, w3, w2, wo, 1024, d // 6).reshape(b, s, d)
 
     return jax.shard_map(local, mesh=mesh,
                          in_specs=(P('dp', None, None), P(), P(), P(None, 'tp'), P(), P('tp', None),

time: 2030 us -> 2020 us (level)
  no operation moved by 1% of the time
where the time goes in v3:
time: 2020 us; the launch traced here: 2010 us
  Pallas kernels  1970 us (98%)
  local copies, waits for them, and re-layouts  49.1 us (2%)
    pallas_call x1, Pallas kernels, _mlp(): pl.pallas_call(functools.partial(_mlp_kernel, nf=nf, nn=nn), grid=(nb, (n...  1710 us
    pallas_call x1, Pallas kernels, _qkv(): pl.pallas_call(functools.partial(_qkv_kernel, mc=mc, nc=nc), grid=(t // t...  155 us
    pallas_call x1, Pallas kernels, _attn(): pl.pallas_call(functools.partial(_attn_kernel, seq=seq, tq=tq, dh=dh, nh=...  99.9 us
    unnamed x1, local copies, waits for them, and re-layouts  49.1 us

profile of v3, /device:TPU:0, one launch (start us, length us, event | category | flops | bytes accessed | tf_op | source)
XLA Modules:
  0.0 2014.6 jit_solution(295774750919012525)
XLA Ops:
  0.0 155.3 %qkv.1 = (bf16[12288,3072]{1,0:T(8,128)(2,1)}, bf16[12288,1024]{1,0:T(8,128)(2,1)}, bf16[12288,512]{1,0:T(8,128)(2,1)}) custom-call(bf16[12288,3072]{1,0:T(8,128)(2,1)} %bitcast.x_ref.x_hbm, f32[1,3072]{1,0:T(1,128)} %bitcast.4, f32[1,3072]{1,0:T(1,128)} %bitcast.5, bf16[3072,1024]{1,0:T(8,128)(2,1)} %wq_ref.1, bf16[3072,512]{1,0:T(8,128)(2,1)} %wkv_ref.1), custom_call_target="tpu_custom_call" | custom-call | flops 115964116992 | bytes 150994944 | tf_op jit(solution)/shard_map/qkv/pallas_call | solution.py:51
  155.3 99.9 %attn.1.o_hbm = bf16[12288,1024]{1,0:T(8,128)(2,1)} custom-call(bf16[12288,1024]{1,0:T(8,128)(2,1)} %get-tuple-element.9.q_ref, bf16[12288,512]{1,0:T(8,128)(2,1)} %get-tuple-element.10.kv_ref), custom_call_target="tpu_custom_call" | custom-call | flops 51539607552 | bytes 50331648 | tf_op jit(solution)/shard_map/attn/pallas_call | solution.py:101
  255.3 1710.2 %mlp.1 = bf16[12288,3072]{1,0:T(8,128)(2,1)} custom-call(bf16[12288,3072]{1,0:T(8,128)(2,1)} %bitcast.x_ref.x_hbm, bf16[12288,3072]{1,0:T(8,128)(2,1)} %get-tuple-element.8.ln_hbm, bf16[12288,1024]{1,0:T(8,128)(2,1)} %attn.1.o_hbm, bf16[3072,6144]{1,0:T(8,128)(2,1)} %w1_hbm.1, bf16[3072,6144]{1,0:T(8,128)(2,1)} %w3_hbm.1, bf16[6144,3072]{1,0:T(8,128)(2,1)} %w2_hbm.1, ...), custom_call_target="tpu_custom_call" | custom-call | flops 1468878815232 | bytes 1610612736 | tf_op jit(solution)/shard_map/mlp/pallas_call | solution.py:400
  1965.5 49.1 %copy.11 = bf16[6,2048,3072]{2,1,0:T(8,128)(2,1)} copy(bf16[6,2048,3072]{2,1,0:T(8,128)(2,1)} %bitcast.3) | data formatting | bytes 150994944
